TPU v7x, 32 devices: a whole 2x2x4 slice. The times are simulated.
32 devices in a mesh: grp: 2 (over x), tile: 16 (over z, y, core).
Axes of the slice: x: 2, y: 2, z: 4, core: 2. Of those that a mesh axis runs over, the one named last changes fastest.
Arguments:
- visibility: bfloat16 [2, 512, 512, 1024], P(None, 'tile', None, 'grp'), may hold values from -3 to 3, as said below
- dish_pair_okay: int32 [512, 512], P('tile'), may hold values 0 or 1
- triangles: int32 [3, 32768], P(None, 'tile'), may hold values from 0 to 511, as said below
Outputs:
- triangle_means: float32 [2, 32768], P(None, 'tile')
- closure_spectrum: float32 [2, 1024], P(None, ('grp', 'tile'))
Inputs may be any that keep to these rules, and one draw needn't show every extreme that they name: Both parts of every visibility lie in -3 to 3. `triangles`: column j belongs to block d = j // 2048 and level k = (j % 2048) // 1024; its first antenna lies in block d (antennas d * 32 to d * 32 + 31), its second in block d XOR 2**k, and its third is any antenna other than the first two.
All inputs are finite; a program needn't handle non-finite values. No bound on the sum of `dish_pair_okay` on one device may be relied on, other than what follows from the above.
Results may differ from a plain program's by a relative error of at most 0.0003.
Values may be sent and summed in bfloat16 or wider, within the bound.
A program may use at most 128 MiB of HBM per device.

v0:
```python
import jax
import jax.numpy as jnp
from jax import lax
from jax.sharding import PartitionSpec as P

RADIO_BANDS = 1024
LEVELS = 2
TRI_LVL = 1024


def swapped(array, axis, stride):
    return lax.ppermute(array, axis, [(i, i ^ 1 << stride) for i in range(lax.axis_size(axis))])


def bispectrum(edge_ab, edge_bc, edge_ac):
    edge_ab = edge_ab.astype(jnp.float32)
    edge_bc = edge_bc.astype(jnp.float32)
    edge_ac = edge_ac.astype(jnp.float32)
    prod_real = edge_ab[0] * edge_bc[0] - edge_ab[1] * edge_bc[1]
    prod_imag = edge_ab[0] * edge_bc[1] + edge_ab[1] * edge_bc[0]
    real_part = prod_real * edge_ac[0] + prod_imag * edge_ac[1]
    imag_part = prod_imag * edge_ac[0] - prod_real * edge_ac[1]
    return (real_part, imag_part)


def pick_pairs(table, flag_table, row_index, col_index):
    dish_rows = table.shape[1]
    dish_cols = table.shape[2]
    channels = table.shape[3]
    planes = table.reshape(2, dish_rows * dish_cols, channels)
    flag_flat = flag_table.reshape(dish_rows * dish_cols)
    flat_index = row_index * dish_cols + col_index
    edges = jnp.take(planes, flat_index, axis=1)
    flags = jnp.take(flag_flat, flat_index, axis=0).astype(jnp.float32)
    return (edges, flags)


def body(visibility, dish_pair_okay, triangles):
    block_rows = visibility.shape[1]
    device = lax.axis_index("tile")
    flag_values = dish_pair_okay.astype(jnp.bfloat16)
    spec_real = jnp.zeros((visibility.shape[3],), jnp.float32)
    spec_imag = jnp.zeros((visibility.shape[3],), jnp.float32)
    spec_norm = jnp.zeros((visibility.shape[3],), jnp.float32)
    level_sums = [None] * LEVELS
    level_order = list(range(LEVELS))
    for level_bit in level_order:
        block = triangles[:, level_bit * TRI_LVL : (level_bit + 1) * TRI_LVL]
        count = block.shape[1]
        partner = jnp.bitwise_xor(device, 1 << level_bit)
        first_local = block[0] - device * block_rows
        second_local = block[1] - partner * block_rows
        vertex_point = block[2]
        own_edges, own_flags = pick_pairs(
            visibility,
            flag_values,
            jnp.concatenate([first_local, first_local]),
            jnp.concatenate([block[1], vertex_point]),
        )
        edge_ab = own_edges[:, :count, :]
        edge_ac = own_edges[:, count:, :]
        weight = own_flags[:count] * own_flags[count:]
        wanted = jnp.stack([second_local, vertex_point])
        asked = swapped(wanted, "tile", level_bit)
        picked, picked_flags = pick_pairs(visibility, flag_values, asked[0], asked[1])
        edge_bc, flag_bc = swapped((picked, picked_flags.astype(jnp.bfloat16)), "tile", level_bit)
        weight = weight * flag_bc.astype(jnp.float32)
        real_part, imag_part = bispectrum(edge_ab, edge_bc, edge_ac)
        weighted_real = weight[:, None] * real_part
        weighted_imag = weight[:, None] * imag_part
        magnitude = weight[:, None] * jnp.sqrt(real_part * real_part + imag_part * imag_part)
        spec_real = spec_real + jnp.sum(weighted_real, 0)
        spec_imag = spec_imag + jnp.sum(weighted_imag, 0)
        spec_norm = spec_norm + jnp.sum(magnitude, 0)
        channel_sums = jnp.stack([jnp.sum(weighted_real, 1), jnp.sum(weighted_imag, 1)])
        level_sums[level_bit] = channel_sums
    joined = jnp.concatenate(level_sums, axis=1)
    joined = lax.psum(joined, "grp")
    triangle_means = joined / RADIO_BANDS
    spec_real, spec_imag, spec_norm = (
        lax.psum_scatter(spec_real, "tile", scatter_dimension=0, tiled=True),
        lax.psum_scatter(spec_imag, "tile", scatter_dimension=0, tiled=True),
        lax.psum_scatter(spec_norm, "tile", scatter_dimension=0, tiled=True),
    )
    closure_spectrum = jnp.stack([spec_real, spec_imag]) / (1.0 + spec_norm)
    return (triangle_means, closure_spectrum)


def solution(mesh):
    placed = (P(None, "tile", None, "grp"), P("tile", None), P(None, "tile"))
    return jax.shard_map(
        body,
        mesh=mesh,
        in_specs=placed,
        out_specs=(P(None, "tile"), P(None, ("grp", "tile"))),
        check_vma=False,
    )
```

profile of v0, /device:TPU:0, one launch (start us, length us, event | category | flops | bytes accessed | tf_op | source)
XLA Modules:
  0.0 339.9 jit_solution(17383575481884709088)
XLA Ops:
  0.6 0.9 broadcast_subtract_fusion.1
  1.6 3.1 collective-permute-start.3
  4.6 0.1 collective-permute-start
  4.7 0.8 convert_bitcast_fusion
  5.6 13.1 %gather_fusion.4 = bf16[2048]{0:T(1024)(128)(2,1)S(1)} fusion(bf16[16384]{0:T(1024)(128)(2,1)S(1)} %bitcast.77, s32[2048]{0:T(1024)S(1)} %broadcast_clamp_fusion), kind=kCustom, calls=%fused_computation.4.clone | custom fusion | bytes 16384 | tf_op jit(solution)/shard_map/jit(_take)/gather | solution.py:34
  18.7 13.1 %gather_fusion = bf16[2048]{0:T(1024)(128)(2,1)S(1)} fusion(bf16[16384]{0:T(1024)(128)(2,1)S(1)} %bitcast.78, s32[2048]{0:T(1024)S(1)} %broadcast_clamp_fusion.1), kind=kCustom, calls=%fused_computation.clone | custom fusion | bytes 16384 | tf_op jit(solution)/shard_map/jit(_take)/gather | solution.py:34
  31.8 60.3 %copy.31 = bf16[2,32,512,512]{3,0,2,1:T(2,128)(2,1)} copy(bf16[2,32,512,512]{3,2,1,0:T(8,128)(2,1)} %param.11) | data formatting | bytes 67108864 | tf_op args[0]
  92.1 38.9 %gather_fusion.6 = bf16[2048,2,512]{2,1,0:T(2,128)(2,1)} fusion(bf16[2,16384,512]{2,0,1:T(2,128)(2,1)} %bitcast.81, s32[2048]{0:T(1024)S(1)} %broadcast_clamp_fusion), kind=kCustom, calls=%fused_computation.6.clone | custom fusion | bytes 8396800 | tf_op jit(solution)/shard_map/jit(_take)/gather | solution.py:33
  131.1 2.9 fusion
  134.0 4.4 %slice_convert_fusion.1 = (f32[2,1024,512]{2,1,0:T(8,128)}, f32[2,1024,512]{2,1,0:T(8,128)}) fusion(bf16[2,2048,512]{2,1,0:T(8,128)(2,1)S(1)} %fusion), kind=kLoop, calls=%fused_computation.13 | loop fusion | flops 2097152 | bytes 12582912 | tf_op jit(solution)/shard_map/convert_element_type | solution.py:16
  138.4 38.9 %gather_fusion.2 = bf16[2048,2,512]{2,1,0:T(2,128)(2,1)} fusion(bf16[2,16384,512]{2,0,1:T(2,128)(2,1)} %bitcast.82, s32[2048]{0:T(1024)S(1)} %broadcast_clamp_fusion.1), kind=kCustom, calls=%fused_computation.2.clone | custom fusion | bytes 8396800 | tf_op jit(solution)/shard_map/jit(_take)/gather | solution.py:33
  177.3 0.0 collective-permute-done.3
  177.3 6.8 %gather_fusion.5 = bf16[1024]{0:T(1024)(128)(2,1)S(1)} fusion(bf16[16384]{0:T(1024)(128)(2,1)S(1)} %bitcast.79, s32[1024]{0:T(1024)S(1)} %fusion.25), kind=kCustom, calls=%fused_computation.5.clone | custom fusion | bytes 8192 | tf_op jit(solution)/shard_map/jit(_take)/gather | solution.py:34
  184.2 19.8 %gather_fusion.7 = bf16[1024,2,512]{2,1,0:T(2,128)(2,1)} fusion(bf16[2,16384,512]{2,0,1:T(2,128)(2,1)} %bitcast.83, s32[1024]{0:T(1024)S(1)} %fusion.25), kind=kCustom, calls=%fused_computation.7.clone | custom fusion | bytes 4198400 | tf_op jit(solution)/shard_map/jit(_take)/gather | solution.py:33
  203.9 0.0 collective-permute-done
  204.0 6.8 %gather_fusion.1 = bf16[1024]{0:T(1024)(128)(2,1)S(1)} fusion(bf16[16384]{0:T(1024)(128)(2,1)S(1)} %bitcast.80, s32[1024]{0:T(1024)S(1)} %fusion.24), kind=kCustom, calls=%fused_computation.1.clone | custom fusion | bytes 8192 | tf_op jit(solution)/shard_map/jit(_take)/gather | solution.py:34
  210.8 14.7 %gather_fusion.3 = bf16[1024,2,512]{2,1,0:T(2,128)(2,1)S(1)} fusion(bf16[2,16384,512]{2,0,1:T(2,128)(2,1)} %bitcast.84, s32[1024]{0:T(1024)S(1)} %fusion.24), kind=kCustom, calls=%fused_computation.3.clone | custom fusion | bytes 4198400 | tf_op jit(solution)/shard_map/jit(_take)/gather | solution.py:33
  225.5 3.3 fusion.10
  228.8 0.1 collective-permute-start.5
  228.8 0.0 copy-start.2
  228.8 1.7 fusion.11
  230.6 0.5 collective-permute-start.2
  231.0 0.7 copy-done.2
  231.8 1.0 fusion.1
  232.8 0.0 copy-start.7
  232.8 0.5 collective-permute-start.1
  233.3 4.4 %slice_convert_fusion.3 = (f32[2,1024,512]{2,1,0:T(8,128)}, f32[2,1024,512]{2,1,0:T(8,128)}) fusion(bf16[2,2048,512]{2,1,0:T(8,128)(2,1)S(1)} %fusion.1), kind=kLoop, calls=%fused_computation.15 | loop fusion | flops 2097152 | bytes 12582912 | tf_op jit(solution)/shard_map/convert_element_type | solution.py:16
  237.8 0.0 copy-done.7
  237.8 0.6 dynamic-slice
  239.0 1.8 collective-permute-start.4
  240.8 0.0 collective-permute-done.1
  240.8 36.3 %collective-permute-done.4 = bf16[1024]{0:T(1024)(128)(2,1)S(1)} collective-permute-done((bf16[1024]{0:T(1024)(128)(2,1)S(1)}, bf16[1024]{0:T(1024)(128)(2,1)S(1)}, u32[]{:S(2)}, u32[]{:S(2)}) %collective-permute-start.4) | collective-permute-done | bytes 2080 | tf_op jit(solution)/shard_map/ppermute | solution.py:12
  277.1 0.0 copy-start
  277.2 0.0 collective-permute-done.5
  277.2 2.3 convert_element_type.46
  279.5 0.5 copy-done
  280.0 0.0 copy-start.3
  280.0 6.0 %multiply_add_fusion = (f32[1,1024,512]{2,1,0:T(8,128)S(1)}, f32[1,1024,512]{2,1,0:T(8,128)}, f32[1,1024,512]{2,1,0:T(8,128)}) fusion(f32[2,1024,512]{2,1,0:T(8,128)S(1)} %copy-done, f32[2,1024,512]{2,1,0:T(8,128)S(1)} %convert_element_type.46, f32[2,1024,512]{2,1,0:T(8,128)} %get-tuple-element.35), kind=kLoop, calls=%fused_computation.37 | loop fusion | flops 4718592 | bytes 18874368 | tf_op jit(solution)/shard_map/add | solution.py:21
  285.9 0.0 copy-start.1
  285.9 0.0 collective-permute-done.2
  285.9 2.3 convert_element_type.41
  288.3 0.0 copy-done.3
  288.3 0.5 copy-done.1
  288.8 4.6 %multiply_add_fusion.2 = (f32[1,1024,512]{2,1,0:T(8,128)}, f32[1,1024,512]{2,1,0:T(8,128)}, f32[1,1024,512]{2,1,0:T(8,128)}) fusion(f32[2,1024,512]{2,1,0:T(8,128)S(1)} %copy-done.1, f32[2,1024,512]{2,1,0:T(8,128)S(1)} %convert_element_type.41, f32[2,1024,512]{2,1,0:T(8,128)S(1)} %copy-done.3), kind=kLoop, calls=%fused_computation.41 | loop fusion | flops 4718592 | bytes 18874368 | tf_op jit(solution)/shard_map/add | solution.py:21
  293.4 0.0 copy-start.4
  293.4 0.0 copy-start.5
  293.4 0.0 copy-start.6
  293.4 3.7 %fusion.5 = (f32[512]{0:T(512)S(1)}, f32[512]{0:T(512)S(1)}, f32[1024]{0:T(1024)S(1)}, f32[512]{0:T(512)S(1)}, f32[1024]{0:T(1024)S(1)}) fusion(f32[1,1024,512]{2,1,0:T(8,128)S(1)} %get-tuple-element.30, f32[1024]{0:T(1024)S(1)} %fusion.22, f32[1,1024,512]{2,1,0:T(8,128)} %get-tuple-element.32, f32[2,1024,512]{2,1,0:T(8,128)S(1)} %copy-done, ...), kind=kLoop, calls=%fused_computation.21 | loop fusion | flops 7336448 | bytes 10504192 | tf_op jit(solution)/shard_map/reduce_sum | solution.py:74
  297.1 0.0 copy-done.4
  297.1 0.0 copy-done.5
  297.2 0.4 copy-done.6
  297.5 2.1 fusion.9
  299.6 8.2 %psum.7 = f32[2,2048]{1,0:T(2,128)S(1)} all-reduce(f32[2,2048]{1,0:T(2,128)S(1)} %maximum_maximum_fusion), channel_id=1, replica_groups=mesh['grp'=2,'tile'=16] {'grp'}, use_global_device_ids=true, to_apply=%region_4.9 | all-reduce | flops 4096 | bytes 32768 | tf_op jit(solution)/shard_map/psum | solution.py:78
  307.8 0.6 broadcast_multiply_fusion
  308.5 30.7 %all-reduce.3 = (f32[512]{0:T(512)S(1)}, f32[512]{0:T(512)S(1)}, f32[512]{0:T(512)S(1)}) all-reduce(f32[512]{0:T(512)S(1)} %add.104, f32[512]{0:T(512)S(1)} %add.103, f32[512]{0:T(512)S(1)} %add.107), channel_id=3, replica_groups=mesh['grp'=2,'tile'=16] {'tile'}, use_global_device_ids=true, to_apply=%region_10.15.clone | all-reduce | flops 1536 | bytes 12288
  339.2 0.1 dynamic-slice_add_fusion
  339.2 0.1 dynamic-slice_bitcast_fusion
  339.3 0.6 maximum_divide_fusion
  (19 shorter events, 0.2 us)
Async XLA Ops:
  1.6 175.8 %collective-permute-start.3 = (s32[2,1024]{1,0:T(2,128)S(1)}, s32[2,1024]{1,0:T(2,128)S(1)}, u32[]{:S(2)}, u32[]{:S(2)}) collective-permute-start(s32[2,1024]{1,0:T(2,128)S(1)} %pad_add_fusion.1), channel_id=1, source_target_pairs={{0,2},{1,3},{2,0},{3,1},{4,6},{5,7},{6,4},{7,5},{8,10},{9,11},{10,... | collective-permute-start | bytes 24584 | tf_op jit(solution)/shard_map/ppermute | solution.py:12
  4.6 199.3 %collective-permute-start = (s32[2,1024]{1,0:T(2,128)S(1)}, s32[2,1024]{1,0:T(2,128)S(1)}, u32[]{:S(2)}, u32[]{:S(2)}) collective-permute-start(s32[2,1024]{1,0:T(2,128)S(1)} %pad_add_fusion), channel_id=1, source_target_pairs={{0,1},{1,0},{2,3},{3,2},{4,5},{5,4},{6,7},{7,6},{8,9},{9,8},{10,11... | collective-permute-start | bytes 24584 | tf_op jit(solution)/shard_map/ppermute | solution.py:12
  228.8 48.4 %collective-permute-start.5 = (bf16[2,1024,512]{2,1,0:T(8,128)(2,1)}, bf16[2,1024,512]{2,1,0:T(8,128)(2,1)}, u32[]{:S(2)}, u32[]{:S(2)}) collective-permute-start(bf16[2,1024,512]{2,1,0:T(8,128)(2,1)} %fusion.10), channel_id=1, source_target_pairs={{0,2},{1,3},{2,0},{3,1},{4,6},{5,7},{6,4},{7,5},{8,10},{9,11},{10,... | collective-permute-start | bytes 6291464 | tf_op jit(solution)/shard_map/ppermute | solution.py:12
  228.8 2.9 copy-start.2
  230.6 55.4 %collective-permute-start.2 = (bf16[2,1024,512]{2,1,0:T(8,128)(2,1)}, bf16[2,1024,512]{2,1,0:T(8,128)(2,1)}, u32[]{:S(2)}, u32[]{:S(2)}) collective-permute-start(bf16[2,1024,512]{2,1,0:T(8,128)(2,1)} %fusion.11), channel_id=1, source_target_pairs={{0,1},{1,0},{2,3},{3,2},{4,5},{5,4},{6,7},{7,6},{8,9},{9,8},{10,11... | collective-permute-start | bytes 6291464 | tf_op jit(solution)/shard_map/ppermute | solution.py:12
  232.8 4.9 %copy-start.7 = (u32[32]{0:T(128)S(1)}, u32[32]{0:T(128)}, u32[]{:S(2)}) copy-start(u32[32]{0:T(128)} %constant.38) | copy-start | bytes 388
  232.8 8.0 %collective-permute-start.1 = (bf16[1024]{0:T(1024)(128)(2,1)S(1)}, bf16[1024]{0:T(1024)(128)(2,1)S(1)}, u32[]{:S(2)}, u32[]{:S(2)}) collective-permute-start(bf16[1024]{0:T(1024)(128)(2,1)S(1)} %get-tuple-element.19), channel_id=1, source_target_pairs={{0,1},{1,0},{2,3},{3,2},{4,5},{5,4},{6,7},{7,6},{8,9},{9,8},{10,11... | collective-permute-start | bytes 6152 | tf_op jit(solution)/shard_map/ppermute | solution.py:12
  239.0 38.2 %collective-permute-start.4 = (bf16[1024]{0:T(1024)(128)(2,1)S(1)}, bf16[1024]{0:T(1024)(128)(2,1)S(1)}, u32[]{:S(2)}, u32[]{:S(2)}) collective-permute-start(bf16[1024]{0:T(1024)(128)(2,1)S(1)} %get-tuple-element.26), channel_id=1, source_target_pairs={{0,2},{1,3},{2,0},{3,1},{4,6},{5,7},{6,4},{7,5},{8,10},{9,11},{10,... | collective-permute-start | bytes 6152 | tf_op jit(solution)/shard_map/ppermute | solution.py:12
  277.1 2.8 copy-start
  280.0 8.3 %copy-start.3 = (f32[2,1024,512]{2,1,0:T(8,128)S(1)}, f32[2,1024,512]{2,1,0:T(8,128)}, u32[]{:S(2)}) copy-start(f32[2,1024,512]{2,1,0:T(8,128)} %get-tuple-element.33) | copy-start | bytes 12582916
  285.9 2.8 copy-start.1
  293.4 3.7 %copy-start.4 = (f32[1,1024,512]{2,1,0:T(8,128)S(1)}, f32[1,1024,512]{2,1,0:T(8,128)}, u32[]{:S(2)}) copy-start(f32[1,1024,512]{2,1,0:T(8,128)} %get-tuple-element.23) | copy-start | bytes 6291460
  293.4 3.8 %copy-start.5 = (f32[1,1024,512]{2,1,0:T(8,128)S(1)}, f32[1,1024,512]{2,1,0:T(8,128)}, u32[]{:S(2)}) copy-start(f32[1,1024,512]{2,1,0:T(8,128)} %get-tuple-element.24) | copy-start | bytes 6291460
  293.4 4.1 %copy-start.6 = (f32[1,1024,512]{2,1,0:T(8,128)S(1)}, f32[1,1024,512]{2,1,0:T(8,128)}, u32[]{:S(2)}) copy-start(f32[1,1024,512]{2,1,0:T(8,128)} %get-tuple-element.25) | copy-start | bytes 6291460
where the time goes:
time: 342 us; the launch traced here: 340 us
  local copies, waits for them, and re-layouts  215 us (63%)
  other arithmetic  42 us (12%)
  blocking collectives  38.9 us (11%)
  waiting for transfers between devices  36.4 us (11%)
  starting transfers between devices  5.96 us (2%)
    gather x4, local copies, waits for them, and re-layouts, pick_pairs(): edges = jnp.take(planes, flat_index, axis=1)  112 us
    unnamed x19, local copies, waits for them, and re-layouts  63 us
    gather x4, local copies, waits for them, and re-layouts, pick_pairs(): flags = jnp.take(flag_flat, flat_index, axis=0).astype(jnp.float32)  39.8 us
    ppermute x6, waiting for transfers between devices, swapped(): lax.ppermute(array, axis, [(i, i ^ 1 << stride) for i in range(lax.axis_s...  36.4 us
    unnamed x1, blocking collectives  30.7 us
    add x2, other arithmetic, bispectrum(): real_part = prod_real * edge_ac[0] + prod_imag * edge_ac[1]  10.6 us
    select_n x4, other arithmetic, pick_pairs(): edges = jnp.take(planes, flat_index, axis=1)  9 us
    convert_element_type x2, other arithmetic, bispectrum(): edge_ab = edge_ab.astype(jnp.float32)  8.79 us
  transfers between devices with their start and end apart: 6, of which 1 were waited for; matrix products, arithmetic and copies ran while one was open for 63% of the time, Pallas kernels for 0%

commit v1 on v0

v1 whole, which is shorter than its diff:
```python
import functools

import jax
import jax.numpy as jnp
from jax import lax
from jax.experimental import pallas as pl
from jax.experimental.pallas import tpu as pltpu
from jax.sharding import PartitionSpec as P

TRI_LVL = 1024
LANES = 128
GATHER = 256
BLOCK = 128


def swapped(array, axis, stride):
    return lax.ppermute(array, axis, [(i, i ^ 1 << stride) for i in range(lax.axis_size(axis))])


def gather_kernel(index, flags, vis, *refs, dishes, phases):
    outs, (table, turn) = refs[: len(phases)], refs[len(phases) :]
    step = pl.program_id(0)
    cols, channels = vis.shape[2], vis.shape[3]
    chunks = channels // LANES
    kinds = 2 * chunks
    blank = dishes * cols
    group = 16
    unroll = turn.shape[0]

    @pl.when(step == 0)
    def _():
        table[blank] = jnp.zeros((kinds, LANES), table.dtype)

    @pl.when(step < dishes)
    def _():
        def turn_rows(it, _):
            for u in range(unroll):
                start = pl.multiple_of((it * unroll + u) * group, group)
                for c in range(chunks):
                    for plane in range(2):
                        x = vis[plane, 0, pl.ds(start, group), pl.ds(c * LANES, LANES)]
                        turn[u, pl.ds(2 * c + plane, group, stride=kinds), :] = x.astype(jnp.float32)
            for u in range(unroll):
                start = (it * unroll + u) * group
                y = turn[u].reshape(group, kinds, LANES)
                table[pl.ds(step * cols + start, group)] = y.astype(table.dtype)
            return 0

        lax.fori_loop(0, cols // (group * unroll), turn_rows, 0)

    first = 0
    for out, count in zip(outs, phases):
        low = dishes + first // GATHER

        @pl.when((step >= low) & (step < low + count // GATHER))
        def _(out=out):
            base = (step - dishes) * GATHER

            def copy_rows(it, _):
                for u in range(16):
                    j = it * 16 + u
                    row = index[base + j]
                    row = jnp.where(flags[row] != 0, row, blank)
                    out[j] = table[row]
                return 0

            lax.fori_loop(0, GATHER // 16, copy_rows, 0)

        first += count


def gather_rows(visibility, flags, index, phases):
    _, dishes, cols, channels = visibility.shape
    kinds = 2 * channels // LANES
    steps = dishes + sum(phases) // GATHER
    out_specs, first = [], dishes
    for count in phases:
        n = count // GATHER
        out_specs.append(
            pl.BlockSpec((GATHER, kinds, LANES), lambda i, lo=first, n=n: (jnp.clip(i - lo, 0, n - 1), 0, 0))
        )
        first += n
    return pl.pallas_call(
        functools.partial(gather_kernel, dishes=dishes, phases=phases),
        grid=(steps,),
        in_specs=[
            pl.BlockSpec(memory_space=pltpu.SMEM),
            pl.BlockSpec(memory_space=pltpu.SMEM),
            pl.BlockSpec((2, 1, cols, channels), lambda i: (0, jnp.minimum(i, dishes - 1), 0, 0)),
        ],
        out_specs=out_specs,
        out_shape=[jax.ShapeDtypeStruct((count, kinds, LANES), visibility.dtype) for count in phases],
        scratch_shapes=[
            pltpu.VMEM((dishes * cols + 1, kinds, LANES), visibility.dtype),
            pltpu.VMEM((4, 16 * kinds, LANES), jnp.float32),
        ],
        compiler_params=pltpu.CompilerParams(
            dimension_semantics=("arbitrary",), vmem_limit_bytes=52 * 1024 * 1024
        ),
        name="gather_rows",
    )(index, flags, visibility)


def triangle_kernel(ab, ac, bc, sums, spec, wide, line):
    kinds = ab.shape[1]
    chunks = kinds // 2
    group = 16

    @pl.when(pl.program_id(0) == 0)
    def _():
        spec[...] = jnp.zeros(spec.shape, spec.dtype)

    def fold(x):
        return x[:8] + x[8:]

    def some(it, acc):
        acc = list(acc)
        for u in range(2):
            start = pl.multiple_of((it * 2 + u) * group, group)
            for e, ref in enumerate((ab, bc, ac)):
                rows = ref[pl.ds(start, group)].astype(jnp.float32)
                wide[u, e] = rows.reshape(group * kinds, LANES)
            total_real = total_imag = None
            for c in range(chunks):
                (a_r, a_i), (b_r, b_i), (c_r, c_i) = [
                    [wide[u, e, pl.ds(2 * c + plane, group, stride=kinds), :] for plane in range(2)]
                    for e in range(3)
                ]
                p_r = a_r * b_r - a_i * b_i
                p_i = a_r * b_i + a_i * b_r
                real = p_r * c_r + p_i * c_i
                imag = p_i * c_r - p_r * c_i
                norm = jnp.sqrt(real * real + imag * imag)
                acc[3 * c] = acc[3 * c] + fold(real)
                acc[3 * c + 1] = acc[3 * c + 1] + fold(imag)
                acc[3 * c + 2] = acc[3 * c + 2] + fold(norm)
                total_real = real if c == 0 else total_real + real
                total_imag = imag if c == 0 else total_imag + imag
            line[0, pl.ds(start, group), :] = total_real
            line[1, pl.ds(start, group), :] = total_imag
        return tuple(acc)

    zero = jnp.zeros((8, LANES), jnp.float32)
    acc = lax.fori_loop(0, BLOCK // (2 * group), some, (zero,) * (3 * chunks))
    for c in range(chunks):
        for part in range(3):
            spec[part, c] = spec[part, c] + acc[3 * c + part]
    ones = jnp.ones((8, LANES), jnp.float32)
    for part in range(2):
        lane_sum = lax.dot_general(
            ones,
            line[part],
            (((1,), (1,)), ((), ())),
            precision=lax.Precision.HIGHEST,
            preferred_element_type=jnp.float32,
        )
        sums[pl.ds(part, 1), :] = lane_sum[:1]


def triangle_sums(own, bc, level):
    count, kinds, _ = bc.shape
    n = count // BLOCK
    block = (BLOCK, kinds, LANES)
    return pl.pallas_call(
        triangle_kernel,
        grid=(n,),
        in_specs=[
            pl.BlockSpec(block, lambda i: (2 * level * n + i, 0, 0)),
            pl.BlockSpec(block, lambda i: ((2 * level + 1) * n + i, 0, 0)),
            pl.BlockSpec(block, lambda i: (i, 0, 0)),
        ],
        out_specs=[
            pl.BlockSpec((2, BLOCK), lambda i: (0, i)),
            pl.BlockSpec((3, kinds // 2, 8, LANES), lambda i: (0, 0, 0, 0)),
        ],
        out_shape=[
            jax.ShapeDtypeStruct((2, count), jnp.float32),
            jax.ShapeDtypeStruct((3, kinds // 2, 8, LANES), jnp.float32),
        ],
        scratch_shapes=[
            pltpu.VMEM((2, 3, 16 * kinds, LANES), jnp.float32),
            pltpu.VMEM((2, BLOCK, LANES), jnp.float32),
        ],
        compiler_params=pltpu.CompilerParams(dimension_semantics=("arbitrary",)),
        name="triangle_sums",
    )(own, own, bc)


def body(visibility, dish_pair_okay, triangles):
    _, block_rows, cols, channels = visibility.shape
    levels = triangles.shape[1] // TRI_LVL
    tiles = lax.axis_size("tile")
    device = lax.axis_index("tile")
    asked, own = [], []
    for level in range(levels):
        block = triangles[:, level * TRI_LVL : (level + 1) * TRI_LVL]
        partner = jnp.bitwise_xor(device, 1 << level)
        first_local = block[0] - device * block_rows
        second_local = block[1] - partner * block_rows
        asked.append(swapped(second_local * cols + block[2], "tile", level))
        own += [first_local * cols + block[1], first_local * cols + block[2]]
    order = list(reversed(range(levels)))
    index = jnp.concatenate([asked[level] for level in order] + own)
    phases = (TRI_LVL,) * levels + (2 * levels * TRI_LVL,)
    *picked, own_rows = gather_rows(visibility, dish_pair_okay.reshape(-1), index, phases)
    arrived = {level: swapped(rows, "tile", level) for level, rows in zip(order, picked)}
    parts = [triangle_sums(own_rows, arrived[level], level) for level in range(levels)]
    joined = lax.psum(jnp.concatenate([sums for sums, _ in parts], axis=1), "grp")
    triangle_means = joined / (channels * lax.axis_size("grp"))
    spec = sum(part for _, part in parts).sum(2).reshape(3, tiles, channels // tiles)
    spec = lax.all_to_all(spec.transpose(1, 0, 2), "tile", 0, 0).sum(0)
    closure_spectrum = spec[:2] / (1.0 + spec[2:])
    return (triangle_means, closure_spectrum)


def solution(mesh):
    placed = (P(None, "tile", None, "grp"), P("tile", None), P(None, "tile"))
    return jax.shard_map(
        body,
        mesh=mesh,
        in_specs=placed,
        out_specs=(P(None, "tile"), P(None, ("grp", "tile"))),
        check_vma=False,
    )
```

time: 342 us -> 140 us (0.41)
  local copies, waits for them, and re-layouts: 215 us -> 2.92 us
  Pallas kernels: 0 us -> 68.1 us
  other arithmetic: 42 us -> 3.68 us
  blocking collectives: 38.9 us -> 8.42 us
  waiting for transfers between devices: 36.4 us -> 44.3 us
  starting transfers between devices: 5.96 us -> 11 us
    gather x8 -> x0, local copies, waits for them, and re-layouts: 152 us -> none  [the longest x4 112 us: pick_pairs(): edges = jnp.take(planes, flat_index, axis=1)]
    pallas_call x0 -> x3, Pallas kernels: none -> 68.1 us  [the longest x1 50.3 us: gather_rows(): pl.pallas_call(functools.partial(gather_kernel, dishes=dishes, phases=pha...]
    unnamed x19 -> x9, local copies, waits for them, and re-layouts: 63 us -> 2.22 us
    unnamed x1 -> x0, blocking collectives: 30.7 us -> none
    convert_element_type x6 -> x0, other arithmetic: 13.5 us -> none  [the longest x2 8.79 us: bispectrum(): edge_ab = edge_ab.astype(jnp.float32)]
    add x8 -> x2, other arithmetic: 10.7 us -> 0.01 us  [body(): asked.append(swapped(second_local * cols + block[2], 'tile', level))]
    select_n x6 -> x0, other arithmetic: 9.02 us -> none  [the longest x4 9 us: pick_pairs(): edges = jnp.take(planes, flat_index, axis=1)]
    all_to_all x0 -> x1, waiting for transfers between devices: none -> 6.02 us  [body(): spec = lax.all_to_all(spec.transpose(1, 0, 2), 'tile', 0, 0).sum(0)]
  transfers between devices with their start and end apart: 6 -> 5, of which waited for: 1 -> 4; matrix products, arithmetic and copies ran while one was open for 63% -> 1% of each run, Pallas kernels for 0% -> 6%
where the time goes in v1:
time: 140 us; the launch traced here: 139 us
  Pallas kernels  68.1 us (49%)
  waiting for transfers between devices  44.3 us (32%)
  starting transfers between devices  11 us (8%)
  blocking collectives  8.42 us (6%)
  other arithmetic  3.68 us (3%)
  local copies, waits for them, and re-layouts  2.92 us (2%)
    pallas_call x1, Pallas kernels, gather_rows(): pl.pallas_call(functools.partial(gather_kernel, dishes=dishes, phases=pha...  50.3 us
    ppermute x4, waiting for transfers between devices, swapped(): lax.ppermute(array, axis, [(i, i ^ 1 << stride) for i in range(lax.axis_s...  38.3 us
    pallas_call x2, Pallas kernels, triangle_sums(): pl.pallas_call(triangle_kernel, grid=(n,), in_specs=[pl.BlockSpec(block,...  17.8 us
    psum x1, blocking collectives, body(): lax.psum(jnp.concatenate([sums for sums, _ in parts], axis=1), 'grp')  8.42 us
    all_to_all x1, waiting for transfers between devices, body(): spec = lax.all_to_all(spec.transpose(1, 0, 2), 'tile', 0, 0).sum(0)  6.02 us
    all_to_all x1, starting transfers between devices, body(): spec = lax.all_to_all(spec.transpose(1, 0, 2), 'tile', 0, 0).sum(0)  5.93 us
    ppermute x4, starting transfers between devices, swapped(): lax.ppermute(array, axis, [(i, i ^ 1 << stride) for i in range(lax.axis_s...  5.09 us
  transfers between devices with their start and end apart: 5, of which 4 were waited for; matrix products, arithmetic and copies ran while one was open for 1% of the time, Pallas kernels for 6%

profile of v1, /device:TPU:0, one launch (start us, length us, event | category | flops | bytes accessed | tf_op | source)
XLA Modules:
  0.0 139.2 jit_solution(15993507344439613388)
XLA Ops:
  0.6 0.9 subtract_multiply_fusion
  1.6 3.1 %collective-permute-start = (s32[1024]{0:T(1024)S(1)}, s32[1024]{0:T(1024)S(1)}, u32[]{:S(2)}, u32[]{:S(2)}) collective-permute-start(s32[1024]{0:T(1024)S(1)} %multiply_add_fusion.1), channel_id=1, source_target_pairs={{0,2},{1,3},{2,0},{3,1},{4,6},{5,7},{6,4},{7,5},{8,10},{9,11},{10,... | collective-permute-start | bytes 12296 | tf_op jit(solution)/shard_map/ppermute | solution.py:17
  4.6 0.0 collective-permute-start.1
  4.6 0.9 copy.6
  5.5 0.7 collective-permute-done
  6.2 0.0 collective-permute-done.1
  6.3 50.3 %gather_rows.1 = (bf16[1024,8,128]{2,1,0:T(8,128)(2,1)}, bf16[1024,8,128]{2,1,0:T(8,128)(2,1)}, bf16[4096,8,128]{2,1,0:T(8,128)(2,1)}) custom-call(s32[6144]{0:T(1024)S(1)} %constant_dynamic-update-slice_fusion.index, s32[16384]{0:T(1024)S(1)} %bitcast.11, bf16[2,32,512,512]{3,2,1,0:T(8,128)(2,1)} %vis.1), custom_call_target="tpu_custom_call" | custom-call | tf_op jit(solution)/shard_map/gather_rows/pallas_call | solution.py:83
  56.5 0.0 collective-permute-start.2
  56.5 2.0 %collective-permute-start.3 = (bf16[1024,8,128]{2,1,0:T(8,128)(2,1)}, bf16[1024,8,128]{2,1,0:T(8,128)(2,1)S(1)}, u32[]{:S(2)}, u32[]{:S(2)}) collective-permute-start(bf16[1024,8,128]{2,1,0:T(8,128)(2,1)} %get-tuple-element.12), channel_id=1, source_target_pairs={{0,2},{1,3},{2,0},{3,1},{4,6},{5,7},{6,4},{7,5},{8,10},{9,11},{10,... | collective-permute-start | bytes 6291464 | tf_op jit(solution)/shard_map/ppermute | solution.py:17
  58.5 2.5 %collective-permute-done.2.bc = bf16[1024,8,128]{2,1,0:T(8,128)(2,1)} collective-permute-done((bf16[1024,8,128]{2,1,0:T(8,128)(2,1)}, bf16[1024,8,128]{2,1,0:T(8,128)(2,1)}, u32[]{:S(2)}, u32[]{:S(2)}) %collective-permute-start.2) | collective-permute-done | bytes 2097184 | tf_op jit(solution)/shard_map/ppermute | solution.py:17
  61.0 8.9 %triangle_sums.2 = (f32[2,1024]{1,0:T(2,128)}, f32[3,4,8,128]{3,2,1,0:T(8,128)}) custom-call(bf16[4096,8,128]{2,1,0:T(8,128)(2,1)} %get-tuple-element.9.ab.ac, bf16[4096,8,128]{2,1,0:T(8,128)(2,1)} %get-tuple-element.9.ab.ac, bf16[1024,8,128]{2,1,0:T(8,128)(2,1)} %collective-permute-done.2.bc), custom_call_target="tpu_custom_call" | custom-call | tf_op jit(solution)/shard_map/triangle_sums/pallas_call | solution.py:164
  70.0 0.0 copy-start.2
  70.0 0.0 copy-start.1
  70.0 35.1 %collective-permute-done.3.bc = bf16[1024,8,128]{2,1,0:T(8,128)(2,1)S(1)} collective-permute-done((bf16[1024,8,128]{2,1,0:T(8,128)(2,1)}, bf16[1024,8,128]{2,1,0:T(8,128)(2,1)S(1)}, u32[]{:S(2)}, u32[]{:S(2)}) %collective-permute-start.3) | collective-permute-done | bytes 2097184 | tf_op jit(solution)/shard_map/ppermute | solution.py:17
  105.1 0.0 copy-start
  105.1 1.3 copy-done
  106.4 8.9 %triangle_sums.3 = (f32[2,1024]{1,0:T(2,128)}, f32[3,4,8,128]{3,2,1,0:T(8,128)}) custom-call(bf16[4096,8,128]{2,1,0:T(8,128)(2,1)} %get-tuple-element.9.ab.ac, bf16[4096,8,128]{2,1,0:T(8,128)(2,1)} %get-tuple-element.9.ab.ac, bf16[1024,8,128]{2,1,0:T(8,128)(2,1)} %copy-done), custom_call_target="tpu_custom_call" | custom-call | tf_op jit(solution)/shard_map/triangle_sums/pallas_call | solution.py:164
  115.3 0.0 copy-done.2
  115.3 0.7 pad_maximum_fusion
  116.0 8.4 %psum.7 = f32[2,2048]{1,0:T(2,128)S(1)} all-reduce(f32[2,2048]{1,0:T(2,128)S(1)} %pad_maximum_fusion), channel_id=1, replica_groups=mesh['grp'=2,'tile'=16] {'grp'}, use_global_device_ids=true, to_apply=%region_0.0 | all-reduce | flops 4096 | bytes 32768 | tf_op jit(solution)/shard_map/psum | solution.py:208
  124.4 0.0 copy-done.1
  124.4 0.8 add_reduce_fusion
  125.3 0.1 reshape.19
  125.3 0.6 copy.5
  126.0 5.9 %all-to-all-start = ((f32[16,3,32]{2,1,0:T(4,128)}), f32[16,3,32]{2,1,0:T(4,128)S(1)}, u32[]{:S(2)}, u32[]{:S(2)}) async-start(f32[16,3,32]{2,1,0:T(4,128)} %copy.5), calls=%async_computation | async-start | bytes 65536 | tf_op jit(solution)/shard_map/all_to_all | solution.py:211
  131.9 0.6 broadcast_multiply_fusion
  132.5 6.0 %all-to-all-done = f32[16,3,32]{2,1,0:T(4,128)S(1)} async-done(((f32[16,3,32]{2,1,0:T(4,128)}), f32[16,3,32]{2,1,0:T(4,128)S(1)}, u32[]{:S(2)}, u32[]{:S(2)}) %all-to-all-start) | async-done | bytes 6176 | tf_op jit(solution)/shard_map/all_to_all | solution.py:211
  138.6 0.6 slice_divide_fusion
  (10 shorter events, 0.1 us)
Async XLA Ops:
  1.6 4.6 %collective-permute-start = (s32[1024]{0:T(1024)S(1)}, s32[1024]{0:T(1024)S(1)}, u32[]{:S(2)}, u32[]{:S(2)}) collective-permute-start(s32[1024]{0:T(1024)S(1)} %multiply_add_fusion.1), channel_id=1, source_target_pairs={{0,2},{1,3},{2,0},{3,1},{4,6},{5,7},{6,4},{7,5},{8,10},{9,11},{10,... | collective-permute-start | bytes 12296 | tf_op jit(solution)/shard_map/ppermute | solution.py:17
  4.6 1.6 %collective-permute-start.1 = (s32[1024]{0:T(1024)S(1)}, s32[1024]{0:T(1024)S(1)}, u32[]{:S(2)}, u32[]{:S(2)}) collective-permute-start(s32[1024]{0:T(1024)S(1)} %multiply_add_fusion), channel_id=1, source_target_pairs={{0,1},{1,0},{2,3},{3,2},{4,5},{5,4},{6,7},{7,6},{8,9},{9,8},{10,11... | collective-permute-start | bytes 12296 | tf_op jit(solution)/shard_map/ppermute | solution.py:17
  56.5 4.5 %collective-permute-start.2 = (bf16[1024,8,128]{2,1,0:T(8,128)(2,1)}, bf16[1024,8,128]{2,1,0:T(8,128)(2,1)}, u32[]{:S(2)}, u32[]{:S(2)}) collective-permute-start(bf16[1024,8,128]{2,1,0:T(8,128)(2,1)} %get-tuple-element.10), channel_id=1, source_target_pairs={{0,1},{1,0},{2,3},{3,2},{4,5},{5,4},{6,7},{7,6},{8,9},{9,8},{10,11... | collective-permute-start | bytes 6291464 | tf_op jit(solution)/shard_map/ppermute | solution.py:17
  56.5 48.5 %collective-permute-start.3 = (bf16[1024,8,128]{2,1,0:T(8,128)(2,1)}, bf16[1024,8,128]{2,1,0:T(8,128)(2,1)S(1)}, u32[]{:S(2)}, u32[]{:S(2)}) collective-permute-start(bf16[1024,8,128]{2,1,0:T(8,128)(2,1)} %get-tuple-element.12), channel_id=1, source_target_pairs={{0,2},{1,3},{2,0},{3,1},{4,6},{5,7},{6,4},{7,5},{8,10},{9,11},{10,... | collective-permute-start | bytes 6291464 | tf_op jit(solution)/shard_map/ppermute | solution.py:17
  70.0 45.4 %copy-start.2 = (f32[2,1024]{1,0:T(2,128)S(1)}, f32[2,1024]{1,0:T(2,128)}, u32[]{:S(2)}) copy-start(f32[2,1024]{1,0:T(2,128)} %get-tuple-element.11) | copy-start | bytes 24580
  70.0 54.5 %copy-start.1 = (f32[3,4,8,128]{3,2,1,0:T(8,128)S(1)}, f32[3,4,8,128]{3,2,1,0:T(8,128)}, u32[]{:S(2)}) copy-start(f32[3,4,8,128]{3,2,1,0:T(8,128)} %get-tuple-element.14) | copy-start | bytes 147460
  105.1 1.4 copy-start
  126.0 12.6 %all-to-all-start = ((f32[16,3,32]{2,1,0:T(4,128)}), f32[16,3,32]{2,1,0:T(4,128)S(1)}, u32[]{:S(2)}, u32[]{:S(2)}) async-start(f32[16,3,32]{2,1,0:T(4,128)} %copy.5), calls=%async_computation | async-start | bytes 65536 | tf_op jit(solution)/shard_map/all_to_all | solution.py:211

commit v2 on v1

--- a/solution.py
+++ b/solution.py
@@ -7,6 +7,7 @@
 from jax.experimental.pallas import tpu as pltpu
 from jax.sharding import PartitionSpec as P
 
+
 TRI_LVL = 1024
 LANES = 128
 GATHER = 256
@@ -17,44 +18,61 @@
     return lax.ppermute(array, axis, [(i, i ^ 1 << stride) for i in range(lax.axis_size(axis))])
 
 
-def gather_kernel(index, flags, vis, *refs, dishes, phases):
-    outs, (table, turn) = refs[: len(phases)], refs[len(phases) :]
+def turn_kernel(vis, table, turn):
     step = pl.program_id(0)
     cols, channels = vis.shape[2], vis.shape[3]
     chunks = channels // LANES
     kinds = 2 * chunks
-    blank = dishes * cols
     group = 16
     unroll = turn.shape[0]
 
     @pl.when(step == 0)
     def _():
-        table[blank] = jnp.zeros((kinds, LANES), table.dtype)
-
-    @pl.when(step < dishes)
-    def _():
-        def turn_rows(it, _):
-            for u in range(unroll):
-                start = pl.multiple_of((it * unroll + u) * group, group)
-                for c in range(chunks):
-                    for plane in range(2):
-                        x = vis[plane, 0, pl.ds(start, group), pl.ds(c * LANES, LANES)]
-                        turn[u, pl.ds(2 * c + plane, group, stride=kinds), :] = x.astype(jnp.float32)
-            for u in range(unroll):
-                start = (it * unroll + u) * group
-                y = turn[u].reshape(group, kinds, LANES)
-                table[pl.ds(step * cols + start, group)] = y.astype(table.dtype)
-            return 0
-
-        lax.fori_loop(0, cols // (group * unroll), turn_rows, 0)
-
+        table[table.shape[0] - 1] = jnp.zeros((kinds, LANES), table.dtype)
+
+    def turn_rows(it, _):
+        for u in range(unroll):
+            start = pl.multiple_of((it * unroll + u) * group, group)
+            for c in range(chunks):
+                for plane in range(2):
+                    x = vis[plane, 0, pl.ds(start, group), pl.ds(c * LANES, LANES)]
+                    turn[u, pl.ds(2 * c + plane, group, stride=kinds), :] = x.astype(jnp.float32)
+        for u in range(unroll):
+            start = (it * unroll + u) * group
+            y = turn[u].reshape(group, kinds, LANES)
+            table[pl.ds(step * cols + start, group)] = y.astype(table.dtype)
+        return 0
+
+    lax.fori_loop(0, cols // (group * unroll), turn_rows, 0)
+
+
+def turned(visibility):
+    _, dishes, cols, channels = visibility.shape
+    kinds = 2 * channels // LANES
+    return pl.pallas_call(
+        turn_kernel,
+        grid=(dishes,),
+        in_specs=[pl.BlockSpec((2, 1, cols, channels), lambda i: (0, i, 0, 0))],
+        out_specs=pl.BlockSpec(memory_space=pltpu.VMEM),
+        out_shape=pltpu.VMEM((dishes * cols + 1, kinds, LANES), visibility.dtype),
+        scratch_shapes=[pltpu.VMEM((4, 16 * kinds, LANES), jnp.float32)],
+        compiler_params=pltpu.CompilerParams(
+            dimension_semantics=("arbitrary",), vmem_limit_bytes=8 * 1024 * 1024
+        ),
+        name="turned",
+    )(visibility)
+
+
+def gather_kernel(index, flags, table, *outs, phases):
+    step = pl.program_id(0)
+    blank = table.shape[0] - 1
     first = 0
     for out, count in zip(outs, phases):
-        low = dishes + first // GATHER
+        low = first // GATHER
 
         @pl.when((step >= low) & (step < low + count // GATHER))
         def _(out=out):
-            base = (step - dishes) * GATHER
+            base = step * GATHER
 
             def copy_rows(it, _):
                 for u in range(16):
@@ -69,11 +87,10 @@
         first += count
 
 
-def gather_rows(visibility, flags, index, phases):
-    _, dishes, cols, channels = visibility.shape
-    kinds = 2 * channels // LANES
-    steps = dishes + sum(phases) // GATHER
-    out_specs, first = [], dishes
+def gather_rows(table, flags, index, phases):
+    kinds = table.shape[1]
+    steps = sum(phases) // GATHER
+    out_specs, first = [], 0
     for count in phases:
         n = count // GATHER
         out_specs.append(
@@ -81,24 +98,19 @@
         )
         first += n
     return pl.pallas_call(
-        functools.partial(gather_kernel, dishes=dishes, phases=phases),
+        functools.partial(gather_kernel, phases=phases),
         grid=(steps,),
         in_specs=[
             pl.BlockSpec(memory_space=pltpu.SMEM),
             pl.BlockSpec(memory_space=pltpu.SMEM),
-            pl.BlockSpec((2, 1, cols, channels), lambda i: (0, jnp.minimum(i, dishes - 1), 0, 0)),
+            pl.BlockSpec(memory_space=pltpu.VMEM),
         ],
         out_specs=out_specs,
-        out_shape=[jax.ShapeDtypeStruct((count, kinds, LANES), visibility.dtype) for count in phases],
-        scratch_shapes=[
-            pltpu.VMEM((dishes * cols + 1, kinds, LANES), visibility.dtype),
-            pltpu.VMEM((4, 16 * kinds, LANES), jnp.float32),
-        ],
+        out_shape=[jax.ShapeDtypeStruct((count, kinds, LANES), table.dtype) for count in phases],
         compiler_params=pltpu.CompilerParams(
-            dimension_semantics=("arbitrary",), vmem_limit_bytes=52 * 1024 * 1024
+            dimension_semantics=("arbitrary",), vmem_limit_bytes=8 * 1024 * 1024
         ),
-        name="gather_rows",
-    )(index, flags, visibility)
+    )(index, flags, table)
 
 
 def triangle_kernel(ab, ac, bc, sums, spec, wide, line):
@@ -157,16 +169,17 @@
         sums[pl.ds(part, 1), :] = lane_sum[:1]
 
 
-def triangle_sums(own, bc, level):
+def triangle_sums(own, bc, first, second):
     count, kinds, _ = bc.shape
     n = count // BLOCK
+    first, second = first // BLOCK, second // BLOCK
     block = (BLOCK, kinds, LANES)
     return pl.pallas_call(
         triangle_kernel,
         grid=(n,),
         in_specs=[
-            pl.BlockSpec(block, lambda i: (2 * level * n + i, 0, 0)),
-            pl.BlockSpec(block, lambda i: ((2 * level + 1) * n + i, 0, 0)),
+            pl.BlockSpec(block, lambda i: (first + i, 0, 0)),
+            pl.BlockSpec(block, lambda i: (second + i, 0, 0)),
             pl.BlockSpec(block, lambda i: (i, 0, 0)),
         ],
         out_specs=[
@@ -186,10 +199,84 @@
     )(own, own, bc)
 
 
+def finish_kernel(*refs, groups, tiles, counts, bands):
+    n = len(counts)
+    sums, specs = refs[:n], refs[n : 2 * n]
+    means, closure, mean_buf, spec_buf, send_g, recv_g, send_t, recv_t = refs[2 * n :]
+    grp, tile = lax.axis_index("grp"), lax.axis_index("tile")
+    chunks = specs[0].shape[1]
+    peers = [(lax.rem(grp + k, groups), tile) for k in range(1, groups)]
+    others = [(grp, lax.rem(tile + k, tiles)) for k in range(1, tiles)]
+    barrier = pltpu.get_barrier_semaphore()
+    for device in peers + others:
+        pl.semaphore_signal(barrier, inc=1, device_id=device, device_id_type=pl.DeviceIdType.MESH)
+    for part in range(3):
+        for c in range(chunks):
+            total = specs[0][part, c]
+            for spec in specs[1:]:
+                total = total + spec[part, c]
+            spec_buf[0, pl.ds(part * chunks + c, 1), :] = jnp.sum(total, 0, keepdims=True)
+    at = 0
+    for ref, count in zip(sums, counts):
+        mean_buf[0, :, pl.ds(at, count)] = ref[...]
+        at += count
+    pl.semaphore_wait(barrier, len(peers) + len(others))
+    copies = []
+    for buf, send, recv, devices in ((mean_buf, send_g, recv_g, peers), (spec_buf, send_t, recv_t, others)):
+        for k, device in enumerate(devices, 1):
+            copy = pltpu.make_async_remote_copy(
+                src_ref=buf.at[0],
+                dst_ref=buf.at[k],
+                send_sem=send.at[k],
+                recv_sem=recv.at[k],
+                device_id=device,
+                device_id_type=pl.DeviceIdType.MESH,
+            )
+            copy.start()
+            copies.append(copy)
+    for copy in copies:
+        copy.wait()
+    total = mean_buf[0]
+    for k in range(1, groups):
+        total = total + mean_buf[k]
+    means[...] = total / bands
+    total = spec_buf[0]
+    for k in range(1, tiles):
+        total = total + spec_buf[k]
+    norm = 1.0 + total[2 * chunks :]
+    closure[pl.ds(0, chunks), :] = total[:chunks] / norm
+    closure[pl.ds(chunks, chunks), :] = total[chunks : 2 * chunks] / norm
+
+
+def finish(sums, specs, groups, tiles, bands):
+    counts = tuple(x.shape[1] for x in sums)
+    chunks = specs[0].shape[1]
+    vmem = pl.BlockSpec(memory_space=pltpu.VMEM)
+    return pl.pallas_call(
+        functools.partial(finish_kernel, groups=groups, tiles=tiles, counts=counts, bands=bands),
+        in_specs=[vmem] * (2 * len(counts)),
+        out_specs=[vmem, vmem],
+        out_shape=[
+            jax.ShapeDtypeStruct((2, sum(counts)), jnp.float32),
+            jax.ShapeDtypeStruct((2 * chunks, LANES), jnp.float32),
+        ],
+        scratch_shapes=[
+            pltpu.VMEM((groups, 2, sum(counts)), jnp.float32),
+            pltpu.VMEM((tiles, 3 * chunks, LANES), jnp.float32),
+            pltpu.SemaphoreType.DMA((groups,)),
+            pltpu.SemaphoreType.DMA((groups,)),
+            pltpu.SemaphoreType.DMA((tiles,)),
+            pltpu.SemaphoreType.DMA((tiles,)),
+        ],
+        compiler_params=pltpu.CompilerParams(collective_id=0, has_side_effects=True),
+        name="finish",
+    )(*sums, *specs)
+
+
 def body(visibility, dish_pair_okay, triangles):
     _, block_rows, cols, channels = visibility.shape
     levels = triangles.shape[1] // TRI_LVL
-    tiles = lax.axis_size("tile")
+    tiles, groups = lax.axis_size("tile"), lax.axis_size("grp")
     device = lax.axis_index("tile")
     asked, own = [], []
     for level in range(levels):
@@ -199,22 +286,40 @@
         second_local = block[1] - partner * block_rows
         asked.append(swapped(second_local * cols + block[2], "tile", level))
         own += [first_local * cols + block[1], first_local * cols + block[2]]
-    order = list(reversed(range(levels)))
-    index = jnp.concatenate([asked[level] for level in order] + own)
-    phases = (TRI_LVL,) * levels + (2 * levels * TRI_LVL,)
-    *picked, own_rows = gather_rows(visibility, dish_pair_okay.reshape(-1), index, phases)
-    arrived = {level: swapped(rows, "tile", level) for level, rows in zip(order, picked)}
-    parts = [triangle_sums(own_rows, arrived[level], level) for level in range(levels)]
-    joined = lax.psum(jnp.concatenate([sums for sums, _ in parts], axis=1), "grp")
-    triangle_means = joined / (channels * lax.axis_size("grp"))
-    spec = sum(part for _, part in parts).sum(2).reshape(3, tiles, channels // tiles)
-    spec = lax.all_to_all(spec.transpose(1, 0, 2), "tile", 0, 0).sum(0)
-    closure_spectrum = spec[:2] / (1.0 + spec[2:])
+    flags = dish_pair_okay.reshape(-1)
+    last = levels - 1
+    near_index = jnp.concatenate(asked[:last] + own)
+    visibility, far_index, near_index, flags = lax.optimization_barrier((visibility, asked[last], near_index, flags))
+    table = turned(visibility)
+    pieces = (GATHER,) * (TRI_LVL // GATHER)
+    far = gather_rows(table, flags, far_index, pieces)
+    far, near_index = lax.optimization_barrier((far, near_index))
+    sent = []
+    for rows in far:
+        sent.append(swapped(rows, "tile", last))
+    far = sent
+    phases = (TRI_LVL,) * last + (2 * levels * TRI_LVL,)
+    *near, own_rows = gather_rows(table, flags, near_index, phases)
+    near = [swapped(rows, "tile", level) for level, rows in enumerate(near)]
+    parts = []
+    for at, rows in [(level * TRI_LVL, rows) for level, rows in enumerate(near)] + [
+        (last * TRI_LVL + k * GATHER, rows) for k, rows in enumerate(far)
+    ]:
+        level, rest = at // TRI_LVL, at % TRI_LVL
+        part = triangle_sums(own_rows, rows, 2 * level * TRI_LVL + rest, (2 * level + 1) * TRI_LVL + rest)
+        own_rows, part = lax.optimization_barrier((own_rows, part))
+        parts.append(part)
+    triangle_means, closure = finish(
+        [sums for sums, _ in parts], [spec for _, spec in parts], groups, tiles, channels * groups
+    )
+    width = channels // tiles
+    closure_spectrum = lax.dynamic_slice_in_dim(closure.reshape(2, channels), device * width, width, 1)
     return (triangle_means, closure_spectrum)
 
 
 def solution(mesh):
     placed = (P(None, "tile", None, "grp"), P("tile", None), P(None, "tile"))
+
     return jax.shard_map(
         body,
         mesh=mesh,

time: 140 us -> 126 us (0.900)
  waiting for transfers between devices: 44.3 us -> 27.7 us
  Pallas kernels: 68.1 us -> 81 us
  blocking collectives: 8.42 us -> 0 us
  local copies, waits for them, and re-layouts: 2.92 us -> 6.72 us
  starting transfers between devices: 11 us -> 7.55 us
  other arithmetic: 3.68 us -> 0.92 us
    ppermute x4 -> x7, waiting for transfers between devices: 38.3 us -> 27.7 us  [swapped(): lax.ppermute(array, axis, [(i, i ^ 1 << stride) for i in range(lax.axis_s...]
    pallas_call x1 -> x4, Pallas kernels: 50.3 us -> 59.4 us  [the longest x1 28.2 us: turned(): pl.pallas_call(turn_kernel, grid=(dishes,), in_specs=[pl.BlockSpec((2, 1,...]
    psum x1 -> x0, blocking collectives: 8.42 us -> none  [body(): lax.psum(jnp.concatenate([sums for sums, _ in parts], axis=1), 'grp')]
    all_to_all x1 -> x0, waiting for transfers between devices: 6.02 us -> none  [body(): spec = lax.all_to_all(spec.transpose(1, 0, 2), 'tile', 0, 0).sum(0)]
    all_to_all x1 -> x0, starting transfers between devices: 5.93 us -> none  [body(): spec = lax.all_to_all(spec.transpose(1, 0, 2), 'tile', 0, 0).sum(0)]
    pallas_call x2 -> x5, Pallas kernels: 17.8 us -> 21.6 us  [triangle_sums(): pl.pallas_call(triangle_kernel, grid=(n,), in_specs=[pl.BlockSpec(block,...]
    unnamed x9 -> x5, local copies, waits for them, and re-layouts: 2.22 us -> 5.4 us
    ppermute x4 -> x7, starting transfers between devices: 5.09 us -> 7.55 us  [swapped(): lax.ppermute(array, axis, [(i, i ^ 1 << stride) for i in range(lax.axis_s...]
  transfers between devices with their start and end apart: 5 -> 7, of which waited for: 4 -> 7; matrix products, arithmetic and copies ran while one was open for 1% -> 1% of each run, Pallas kernels for 6% -> 15%
where the time goes in v2:
time: 126 us; the launch traced here: 125 us
  Pallas kernels  81 us (64%)
  waiting for transfers between devices  27.7 us (22%)
  starting transfers between devices  7.55 us (6%)
  local copies, waits for them, and re-layouts  6.72 us (5%)
    pallas_call x1, Pallas kernels, turned(): pl.pallas_call(turn_kernel, grid=(dishes,), in_specs=[pl.BlockSpec((2, 1,...  28.2 us
    ppermute x7, waiting for transfers between devices, swapped(): lax.ppermute(array, axis, [(i, i ^ 1 << stride) for i in range(lax.axis_s...  27.7 us
    pallas_call x5, Pallas kernels, triangle_sums(): pl.pallas_call(triangle_kernel, grid=(n,), in_specs=[pl.BlockSpec(block,...  21.6 us
    pallas_call x2, Pallas kernels, gather_rows(): pl.pallas_call(functools.partial(gather_kernel, phases=phases), grid=(ste...  21.3 us
    pallas_call x1, Pallas kernels, finish(): pl.pallas_call(functools.partial(finish_kernel, groups=groups, tiles=tile...  9.9 us
    ppermute x7, starting transfers between devices, swapped(): lax.ppermute(array, axis, [(i, i ^ 1 << stride) for i in range(lax.axis_s...  7.55 us
    unnamed x5, local copies, waits for them, and re-layouts  5.4 us
  transfers between devices with their start and end apart: 7, of which 7 were waited for; matrix products, arithmetic and copies ran while one was open for 1% of the time, Pallas kernels for 15%

profile of v2, /device:TPU:0, one launch (start us, length us, event | category | flops | bytes accessed | tf_op | source)
XLA Modules:
  0.0 124.6 jit_solution(9004957188721983595)
XLA Ops:
  0.6 0.9 subtract_multiply_fusion
  1.5 0.6 collective-permute-start.1
  2.1 0.8 collective-permute-done.1
  3.0 2.9 %collective-permute-start = (s32[1024]{0:T(1024)S(1)}, s32[1024]{0:T(1024)S(1)}, u32[]{:S(2)}, u32[]{:S(2)}) collective-permute-start(s32[1024]{0:T(1024)S(1)} %get-tuple-element.91), channel_id=1, source_target_pairs={{0,2},{1,3},{2,0},{3,1},{4,6},{5,7},{6,4},{7,5},{8,10},{9,11},{10,... | collective-permute-start | bytes 12296 | tf_op jit(solution)/shard_map/ppermute | solution.py:18
  5.9 0.9 copy.5
  6.7 0.7 collective-permute-done.index
  7.5 28.2 %turned.1.table = bf16[16385,8,128]{2,1,0:T(8,128)(2,1)S(1)} custom-call(bf16[2,32,512,512]{3,2,1,0:T(8,128)(2,1)} %vis), custom_call_target="tpu_custom_call" | custom-call | tf_op jit(solution)/shard_map/turned/pallas_call | solution.py:52
  35.7 5.5 %shard_map.50 = (bf16[256,8,128]{2,1,0:T(8,128)(2,1)}, bf16[256,8,128]{2,1,0:T(8,128)(2,1)}, bf16[256,8,128]{2,1,0:T(8,128)(2,1)S(1)}, bf16[256,8,128]{2,1,0:T(8,128)(2,1)S(1)}) custom-call(s32[1024]{0:T(1024)S(1)} %collective-permute-done.index, s32[16384]{0:T(1024)S(1)} %bitcast.8, bf16[16385,8,128]{2,1,0:T(8,128)(2,1)S(1)} %turned.1.table), custom_call_target="tpu_custom_call" | custom-call | tf_op jit(solution)/shard_map/pallas_call | solution.py:100
  41.2 15.7 %shard_map.51 = (bf16[1024,8,128]{2,1,0:T(8,128)(2,1)S(1)}, bf16[4096,8,128]{2,1,0:T(8,128)(2,1)S(1)}) custom-call(s32[5120]{0:T(1024)S(1)} %get-tuple-element.51.index, s32[16384]{0:T(1024)S(1)} %bitcast.9, bf16[16385,8,128]{2,1,0:T(8,128)(2,1)S(1)} %turned.1.table), custom_call_target="tpu_custom_call" | custom-call | tf_op jit(solution)/shard_map/pallas_call | solution.py:100
  57.0 0.0 copy-start
  57.0 3.2 %copy-done = bf16[4096,8,128]{2,1,0:T(8,128)(2,1)} copy-done((bf16[4096,8,128]{2,1,0:T(8,128)(2,1)}, bf16[4096,8,128]{2,1,0:T(8,128)(2,1)S(1)}, u32[]{:S(2)}) %copy-start) | copy-done | bytes 8388632
  60.2 0.0 collective-permute-start.2
  60.2 2.0 %collective-permute-start.3 = (bf16[256,8,128]{2,1,0:T(8,128)(2,1)}, bf16[256,8,128]{2,1,0:T(8,128)(2,1)}, u32[]{:S(2)}, u32[]{:S(2)}) collective-permute-start(bf16[256,8,128]{2,1,0:T(8,128)(2,1)} %get-tuple-element.58), channel_id=1, source_target_pairs={{0,2},{1,3},{2,0},{3,1},{4,6},{5,7},{6,4},{7,5},{8,10},{9,11},{10,... | collective-permute-start | bytes 1572872 | tf_op jit(solution)/shard_map/ppermute | solution.py:18
  62.2 0.0 collective-permute-start.4
  62.2 2.0 %collective-permute-start.5 = (bf16[256,8,128]{2,1,0:T(8,128)(2,1)S(1)}, bf16[256,8,128]{2,1,0:T(8,128)(2,1)}, u32[]{:S(2)}, u32[]{:S(2)}) collective-permute-start(bf16[256,8,128]{2,1,0:T(8,128)(2,1)S(1)} %get-tuple-element.68), channel_id=1, source_target_pairs={{0,2},{1,3},{2,0},{3,1},{4,6},{5,7},{6,4},{7,5},{8,10},{9,11},{10,... | collective-permute-start | bytes 1572872 | tf_op jit(solution)/shard_map/ppermute | solution.py:18
  64.2 0.0 collective-permute-start.6
  64.3 0.2 collective-permute-done.2.bc
  64.5 8.9 %triangle_sums.5 = (f32[2,1024]{1,0:T(2,128)}, f32[3,4,8,128]{3,2,1,0:T(8,128)}) custom-call(bf16[4096,8,128]{2,1,0:T(8,128)(2,1)} %copy-done, bf16[4096,8,128]{2,1,0:T(8,128)(2,1)} %copy-done, bf16[1024,8,128]{2,1,0:T(8,128)(2,1)} %collective-permute-done.2.bc), custom_call_target="tpu_custom_call" | custom-call | tf_op jit(solution)/shard_map/triangle_sums/pallas_call | solution.py:177
  73.4 1.9 %collective-permute-done.3.bc = bf16[256,8,128]{2,1,0:T(8,128)(2,1)} collective-permute-done((bf16[256,8,128]{2,1,0:T(8,128)(2,1)}, bf16[256,8,128]{2,1,0:T(8,128)(2,1)}, u32[]{:S(2)}, u32[]{:S(2)}) %collective-permute-start.3) | collective-permute-done | bytes 524320 | tf_op jit(solution)/shard_map/ppermute | solution.py:18
  75.3 3.1 %triangle_sums.6 = (f32[2,256]{1,0:T(2,128)}, f32[3,4,8,128]{3,2,1,0:T(8,128)}) custom-call(bf16[4096,8,128]{2,1,0:T(8,128)(2,1)} %copy-done, bf16[4096,8,128]{2,1,0:T(8,128)(2,1)} %copy-done, bf16[256,8,128]{2,1,0:T(8,128)(2,1)} %collective-permute-done.3.bc), custom_call_target="tpu_custom_call" | custom-call | tf_op jit(solution)/shard_map/triangle_sums/pallas_call | solution.py:177
  78.4 8.1 %collective-permute-done.4.bc = bf16[256,8,128]{2,1,0:T(8,128)(2,1)} collective-permute-done((bf16[256,8,128]{2,1,0:T(8,128)(2,1)}, bf16[256,8,128]{2,1,0:T(8,128)(2,1)}, u32[]{:S(2)}, u32[]{:S(2)}) %collective-permute-start.4) | collective-permute-done | bytes 524320 | tf_op jit(solution)/shard_map/ppermute | solution.py:18
  86.5 3.2 %triangle_sums.7 = (f32[2,256]{1,0:T(2,128)}, f32[3,4,8,128]{3,2,1,0:T(8,128)}) custom-call(bf16[4096,8,128]{2,1,0:T(8,128)(2,1)} %copy-done, bf16[4096,8,128]{2,1,0:T(8,128)(2,1)} %copy-done, bf16[256,8,128]{2,1,0:T(8,128)(2,1)} %collective-permute-done.4.bc), custom_call_target="tpu_custom_call" | custom-call | tf_op jit(solution)/shard_map/triangle_sums/pallas_call | solution.py:177
  89.7 8.1 %collective-permute-done.5.bc = bf16[256,8,128]{2,1,0:T(8,128)(2,1)} collective-permute-done((bf16[256,8,128]{2,1,0:T(8,128)(2,1)S(1)}, bf16[256,8,128]{2,1,0:T(8,128)(2,1)}, u32[]{:S(2)}, u32[]{:S(2)}) %collective-permute-start.5) | collective-permute-done | bytes 524320 | tf_op jit(solution)/shard_map/ppermute | solution.py:18
  97.8 3.2 %triangle_sums.8 = (f32[2,256]{1,0:T(2,128)}, f32[3,4,8,128]{3,2,1,0:T(8,128)}) custom-call(bf16[4096,8,128]{2,1,0:T(8,128)(2,1)} %copy-done, bf16[4096,8,128]{2,1,0:T(8,128)(2,1)} %copy-done, bf16[256,8,128]{2,1,0:T(8,128)(2,1)} %collective-permute-done.5.bc), custom_call_target="tpu_custom_call" | custom-call | tf_op jit(solution)/shard_map/triangle_sums/pallas_call | solution.py:177
  101.0 7.9 %collective-permute-done.6.bc = bf16[256,8,128]{2,1,0:T(8,128)(2,1)} collective-permute-done((bf16[256,8,128]{2,1,0:T(8,128)(2,1)S(1)}, bf16[256,8,128]{2,1,0:T(8,128)(2,1)}, u32[]{:S(2)}, u32[]{:S(2)}) %collective-permute-start.6) | collective-permute-done | bytes 524320 | tf_op jit(solution)/shard_map/ppermute | solution.py:18
  108.8 3.2 %triangle_sums.9 = (f32[2,256]{1,0:T(2,128)}, f32[3,4,8,128]{3,2,1,0:T(8,128)}) custom-call(bf16[4096,8,128]{2,1,0:T(8,128)(2,1)} %copy-done, bf16[4096,8,128]{2,1,0:T(8,128)(2,1)} %copy-done, bf16[256,8,128]{2,1,0:T(8,128)(2,1)} %collective-permute-done.6.bc), custom_call_target="tpu_custom_call" | custom-call | tf_op jit(solution)/shard_map/triangle_sums/pallas_call | solution.py:177
  112.0 9.9 %finish.1 = (f32[2,2048]{1,0:T(2,128)}, f32[8,128]{1,0:T(8,128)}) custom-call(f32[2,1024]{1,0:T(2,128)} %get-tuple-element.56.refs_0_, f32[2,256]{1,0:T(2,128)} %get-tuple-element.61.refs_1_, f32[2,256]{1,0:T(2,128)} %get-tuple-element.66.refs_2_, f32[2,256]{1,0:T(2,128)} %get-tuple-element.71.refs_3_, f32[2,256]{1,0:T(2,128)} %get-tuple-element.76.refs_4_, ...), custom_call_target="tpu_custom_call" | custom-call | tf_op jit(solution)/shard_map/finish/pallas_call | solution.py:255
  121.9 0.7 reshape.19
  122.6 0.6 constant_dynamic-slice_fusion
  123.3 1.3 %copy.11 = f32[2,2048]{1,0:T(2,128)} copy(f32[2,2048]{1,0:T(2,128)} %get-tuple-element.94) | data formatting | bytes 32768
  (6 shorter events, 0.0 us)
Async XLA Ops:
  1.5 1.4 %collective-permute-start.1 = (s32[1024]{0:T(1024)S(1)}, s32[1024]{0:T(1024)S(1)}, u32[]{:S(2)}, u32[]{:S(2)}) collective-permute-start(s32[1024]{0:T(1024)S(1)} %multiply_add_fusion), channel_id=1, source_target_pairs={{0,1},{1,0},{2,3},{3,2},{4,5},{5,4},{6,7},{7,6},{8,9},{9,8},{10,11... | collective-permute-start | bytes 12296 | tf_op jit(solution)/shard_map/ppermute | solution.py:18
  3.0 4.5 %collective-permute-start = (s32[1024]{0:T(1024)S(1)}, s32[1024]{0:T(1024)S(1)}, u32[]{:S(2)}, u32[]{:S(2)}) collective-permute-start(s32[1024]{0:T(1024)S(1)} %get-tuple-element.91), channel_id=1, source_target_pairs={{0,2},{1,3},{2,0},{3,1},{4,6},{5,7},{6,4},{7,5},{8,10},{9,11},{10,... | collective-permute-start | bytes 12296 | tf_op jit(solution)/shard_map/ppermute | solution.py:18
  57.0 3.2 %copy-start = (bf16[4096,8,128]{2,1,0:T(8,128)(2,1)}, bf16[4096,8,128]{2,1,0:T(8,128)(2,1)S(1)}, u32[]{:S(2)}) copy-start(bf16[4096,8,128]{2,1,0:T(8,128)(2,1)S(1)} %get-tuple-element.72.ab.ac) | copy-start | bytes 25165828
  60.2 4.3 %collective-permute-start.2 = (bf16[1024,8,128]{2,1,0:T(8,128)(2,1)S(1)}, bf16[1024,8,128]{2,1,0:T(8,128)(2,1)}, u32[]{:S(2)}, u32[]{:S(2)}) collective-permute-start(bf16[1024,8,128]{2,1,0:T(8,128)(2,1)S(1)} %get-tuple-element.53), channel_id=1, source_target_pairs={{0,1},{1,0},{2,3},{3,2},{4,5},{5,4},{6,7},{7,6},{8,9},{9,8},{10,11... | collective-permute-start | bytes 6291464 | tf_op jit(solution)/shard_map/ppermute | solution.py:18
  60.2 15.1 %collective-permute-start.3 = (bf16[256,8,128]{2,1,0:T(8,128)(2,1)}, bf16[256,8,128]{2,1,0:T(8,128)(2,1)}, u32[]{:S(2)}, u32[]{:S(2)}) collective-permute-start(bf16[256,8,128]{2,1,0:T(8,128)(2,1)} %get-tuple-element.58), channel_id=1, source_target_pairs={{0,2},{1,3},{2,0},{3,1},{4,6},{5,7},{6,4},{7,5},{8,10},{9,11},{10,... | collective-permute-start | bytes 1572872 | tf_op jit(solution)/shard_map/ppermute | solution.py:18
  62.2 24.3 %collective-permute-start.4 = (bf16[256,8,128]{2,1,0:T(8,128)(2,1)}, bf16[256,8,128]{2,1,0:T(8,128)(2,1)}, u32[]{:S(2)}, u32[]{:S(2)}) collective-permute-start(bf16[256,8,128]{2,1,0:T(8,128)(2,1)} %get-tuple-element.63), channel_id=1, source_target_pairs={{0,2},{1,3},{2,0},{3,1},{4,6},{5,7},{6,4},{7,5},{8,10},{9,11},{10,... | collective-permute-start | bytes 1572872 | tf_op jit(solution)/shard_map/ppermute | solution.py:18
  62.2 35.5 %collective-permute-start.5 = (bf16[256,8,128]{2,1,0:T(8,128)(2,1)S(1)}, bf16[256,8,128]{2,1,0:T(8,128)(2,1)}, u32[]{:S(2)}, u32[]{:S(2)}) collective-permute-start(bf16[256,8,128]{2,1,0:T(8,128)(2,1)S(1)} %get-tuple-element.68), channel_id=1, source_target_pairs={{0,2},{1,3},{2,0},{3,1},{4,6},{5,7},{6,4},{7,5},{8,10},{9,11},{10,... | collective-permute-start | bytes 1572872 | tf_op jit(solution)/shard_map/ppermute | solution.py:18
  64.2 44.6 %collective-permute-start.6 = (bf16[256,8,128]{2,1,0:T(8,128)(2,1)S(1)}, bf16[256,8,128]{2,1,0:T(8,128)(2,1)}, u32[]{:S(2)}, u32[]{:S(2)}) collective-permute-start(bf16[256,8,128]{2,1,0:T(8,128)(2,1)S(1)} %get-tuple-element.73), channel_id=1, source_target_pairs={{0,2},{1,3},{2,0},{3,1},{4,6},{5,7},{6,4},{7,5},{8,10},{9,11},{10,... | collective-permute-start | bytes 1572872 | tf_op jit(solution)/shard_map/ppermute | solution.py:18
